TPU v7x, 32 devices: a whole 2x2x4 slice. The times are simulated.
32 devices in a mesh: dp: 16 (over z, x, core), tensor: 2 (over y).
Axes of the slice: x: 2, y: 2, z: 4, core: 2. Of those that a mesh axis runs over, the one named last changes fastest.
Arguments:
- inputs: bfloat16 [64, 320, 1024], P(('dp', 'tensor')), may hold values from -6 to 6
- lengths: int32 [64], P('dp'), may hold values from 224 to 320, as said below
- cotangent: bfloat16 [64, 320, 1024], P(('dp', 'tensor')), may hold values from -6 to 6
- first_gain: bfloat16 [1024], P(('dp', 'tensor')), may hold values from 0.25 to 1.75
- first_shift: bfloat16 [1024], P(('dp', 'tensor')), may hold values from -2 to 2
- qkv_weight: bfloat16 [3, 1024, 1024], P(None, 'dp', 'tensor'), may hold values from -0.1875 to 0.1875
- query_bias: bfloat16 [1024], P(('dp', 'tensor')), may hold values from -3 to 3
- value_bias: bfloat16 [1024], P(('dp', 'tensor')), may hold values from -3 to 3
- out_weight: bfloat16 [1024, 1024], P('tensor', 'dp'), may hold values from -1.5 to 1.5
- out_bias: bfloat16 [1024], P(('dp', 'tensor')), may hold values from -3 to 3
- second_gain: bfloat16 [1024], P(('dp', 'tensor')), may hold values from 0.25 to 1.75
- second_shift: bfloat16 [1024], P(('dp', 'tensor')), may hold values from -2 to 2
- up_weight: bfloat16 [1024, 4096], P('dp', 'tensor'), may hold values from -0.1875 to 0.1875
- up_bias: bfloat16 [4096], P(('dp', 'tensor')), may hold values from -3 to 3
- down_weight: bfloat16 [4096, 1024], P('tensor', 'dp'), may hold values from -0.09375 to 0.09375
- down_bias: bfloat16 [1024], P(('dp', 'tensor')), may hold values from -3 to 3
Outputs:
- output: bfloat16 [64, 320, 1024], P(('dp', 'tensor'))
- input_grad: float32 [64, 320, 1024], P(('dp', 'tensor'))
- first_gain_grad: float32 [1024], P(('dp', 'tensor'))
- first_shift_grad: float32 [1024], P(('dp', 'tensor'))
- qkv_weight_grad: float32 [3, 1024, 1024], P(None, 'dp', 'tensor')
- query_bias_grad: float32 [1024], P(('dp', 'tensor'))
- value_bias_grad: float32 [1024], P(('dp', 'tensor'))
- out_weight_grad: float32 [1024, 1024], P('tensor', 'dp')
- out_bias_grad: float32 [1024], P(('dp', 'tensor'))
- second_gain_grad: float32 [1024], P(('dp', 'tensor'))
- second_shift_grad: float32 [1024], P(('dp', 'tensor'))
- up_weight_grad: float32 [1024, 4096], P('dp', 'tensor')
- up_bias_grad: float32 [4096], P(('dp', 'tensor'))
- down_weight_grad: float32 [4096, 1024], P('tensor', 'dp')
- down_bias_grad: float32 [1024], P(('dp', 'tensor'))
Inputs may be any that keep to these rules, and one draw needn't show every extreme that they name: lengths holds the number of valid slots of each image, counted from its first slot; slots from there on are padding.
All inputs are finite; a program needn't handle non-finite values.
Results may differ from a plain program's by a relative error of at most 0.017.
Values may be sent and summed in bfloat16 or wider, within the bound.
A program may use at most 192 MiB of HBM per device.

v0:
```python
import jax
import jax.numpy as jnp
from jax import lax
from jax.sharding import PartitionSpec as P

HEAD_DIM = 64
EPSILON = 1e-06
BOTH = ("dp", "tensor")
bf16 = jnp.bfloat16
f32 = jnp.float32


def exact_gelu(values):
    return jax.nn.gelu(values, approximate=False)


def norm_stats(values):
    average = jnp.mean(values, axis=-1, keepdims=True)
    centered = values - average
    variance = jnp.mean(centered * centered, axis=-1, keepdims=True)
    scale = lax.rsqrt(variance + EPSILON)
    return (centered * scale, scale)


def norm_back(grad, unit, scale, gain):
    z = grad * gain
    mean_z = jnp.mean(z, axis=-1, keepdims=True)
    mean_zx = jnp.mean(z * unit, axis=-1, keepdims=True)
    return scale * (z - mean_z - unit * mean_zx)


def gather_matrix(shard):
    wide = lax.all_gather(shard, "tensor", axis=1, tiled=True)
    return lax.all_gather(wide, "dp", axis=0, tiled=True)


def scatter_matrix(grad):
    rows, columns = grad.shape
    halves = jnp.stack(jnp.split(grad, lax.axis_size("tensor"), axis=1))
    halves = halves.reshape(-1, columns // lax.axis_size("tensor"))
    return lax.psum_scatter(halves, ("tensor", "dp"), scatter_dimension=0, tiled=True)


def mm(a, b, dims):
    return lax.dot_general(a, b, (dims, ((), ())), preferred_element_type=f32)


NN = ((1,), (0,))
NT = ((1,), (1,))
TN = ((0,), (0,))


def shards(
    inputs,
    lengths,
    cotangent,
    first_gain,
    first_shift,
    qkv_weight,
    query_bias,
    value_bias,
    out_weight,
    out_bias,
    second_gain,
    second_shift,
    up_weight,
    up_bias,
    down_weight,
    down_bias,
):
    image_count, slot_count, width = inputs.shape
    tensor_rank = lax.axis_index("tensor")
    heads = width // HEAD_DIM
    tokens = image_count * slot_count
    score_scale = HEAD_DIM ** (-0.5)
    device_count = lax.axis_size("dp") * lax.axis_size("tensor")
    vectors = (
        first_gain,
        first_shift,
        query_bias,
        value_bias,
        out_bias,
        second_gain,
        second_shift,
        down_bias,
        up_bias,
    )
    sizes = [v.shape[0] for v in vectors]
    packed = lax.all_gather(jnp.concatenate(vectors), BOTH, axis=0)
    full = []
    start = 0
    for size in sizes:
        full.append(packed[:, start : start + size].reshape(-1).astype(f32))
        start += size
    gain_one, shift_one, qbias, vbias, obias, gain_two, shift_two, dbias, ubias = full
    query_w = gather_matrix(qkv_weight[0])
    key_w = gather_matrix(qkv_weight[1])
    value_w = gather_matrix(qkv_weight[2])
    out_t = gather_matrix(out_weight.T)
    up_w = gather_matrix(up_weight)
    down_t = gather_matrix(down_weight.T)
    positions = jnp.arange(slot_count, dtype=jnp.int32)
    own_lengths = lax.dynamic_slice_in_dim(lengths, tensor_rank * image_count, image_count)
    valid = positions[None, :] < own_lengths[:, None]
    valid_rows = valid.astype(f32).reshape(tokens, 1)
    masked = inputs.reshape(tokens, width).astype(f32) * valid_rows
    unit_one, scale_one = norm_stats(masked)
    first = (unit_one * gain_one + shift_one).astype(bf16)

    def split(rows):
        return rows.reshape(image_count, slot_count, heads, HEAD_DIM)

    query = split((mm(first, query_w, NN) + qbias).astype(bf16))
    key = split(mm(first, key_w, NN).astype(bf16))
    value = split((mm(first, value_w, NN) + vbias).astype(bf16))
    scores = jnp.einsum("bqhc,bkhc->bhqk", query, key, preferred_element_type=f32) * score_scale
    scores = jnp.where(valid[:, None, None, :], scores, -1000000000.0)
    highest = jnp.max(scores, axis=-1, keepdims=True)
    shifted = jnp.exp(scores - highest)
    probs = shifted / jnp.sum(shifted, axis=-1, keepdims=True)
    weights_low = probs.astype(bf16)
    mixed = jnp.einsum("bhqk,bkhc->bqhc", weights_low, value, preferred_element_type=f32)
    mixed = mixed.astype(bf16).reshape(tokens, width)
    middle = masked + mm(mixed, out_t, NT) + obias
    unit_two, scale_two = norm_stats(middle)
    second = (unit_two * gain_two + shift_two).astype(bf16)
    hidden = mm(second, up_w, NN) + ubias
    active = exact_gelu(hidden).astype(bf16)
    output = (middle + mm(active, down_t, NT) + dbias).astype(bf16)
    grad_low = cotangent.reshape(tokens, width)
    grad_out = grad_low.astype(f32)
    down_grad = scatter_matrix(mm(grad_low, active, TN).astype(bf16))
    grad_active = mm(grad_low, down_t, NN)
    grad_hidden32 = jax.vjp(exact_gelu, hidden)[1](grad_active)[0]
    grad_hidden = grad_hidden32.astype(bf16)
    up_grad = scatter_matrix(mm(second, grad_hidden, TN).astype(bf16))
    grad_second = mm(grad_hidden, up_w, NT)
    grad_middle = grad_out + norm_back(grad_second, unit_two, scale_two, gain_two)
    grad_attn = grad_middle.astype(bf16)
    out_grad = scatter_matrix(mm(grad_attn, mixed, TN).astype(bf16))
    grad_mixed = split(mm(grad_attn, out_t, NN).astype(bf16))
    grad_weights = jnp.einsum("bqhc,bkhc->bhqk", grad_mixed, value, preferred_element_type=f32)
    value_grad = jnp.einsum("bhqk,bqhc->bkhc", weights_low, grad_mixed, preferred_element_type=f32)
    value_grad = value_grad.astype(bf16).reshape(tokens, width)
    inner = jnp.sum(probs * grad_weights, axis=-1, keepdims=True)
    grad_scores = (probs * (grad_weights - inner)).astype(bf16)
    query_grad = (
        jnp.einsum("bhqk,bkhc->bqhc", grad_scores, key, preferred_element_type=f32) * score_scale
    )
    key_grad = (
        jnp.einsum("bhqk,bqhc->bkhc", grad_scores, query, preferred_element_type=f32) * score_scale
    )
    query_grad = query_grad.astype(bf16).reshape(tokens, width)
    key_grad = key_grad.astype(bf16).reshape(tokens, width)
    qkv_grad = jnp.stack(
        [
            scatter_matrix(mm(first, query_grad, TN).astype(bf16)),
            scatter_matrix(mm(first, key_grad, TN).astype(bf16)),
            scatter_matrix(mm(first, value_grad, TN).astype(bf16)),
        ]
    )
    grad_first = mm(query_grad, query_w, NT) + mm(key_grad, key_w, NT) + mm(value_grad, value_w, NT)
    grad_in = norm_back(grad_first, unit_one, scale_one, gain_one)
    input_grad = (grad_middle + grad_in) * valid_rows

    def total(values):
        return jnp.sum(values.astype(f32), axis=0)

    vector_grads = (
        total(grad_first * unit_one),
        total(grad_first),
        total(query_grad),
        total(value_grad),
        total(grad_attn),
        total(grad_second * unit_two),
        total(grad_second),
        total(grad_low),
        total(grad_hidden),
    )
    stacked = jnp.concatenate([v.reshape(device_count, -1) for v in vector_grads], axis=1)
    own = lax.psum_scatter(stacked, BOTH, scatter_dimension=0, tiled=True)[0]
    shares = []
    start = 0
    for size in sizes:
        shares.append(own[start : start + size])
        start += size
    return (
        output.reshape(inputs.shape),
        input_grad.reshape(inputs.shape),
        shares[0],
        shares[1],
        qkv_grad.astype(f32),
        shares[2],
        shares[3],
        out_grad.T.astype(f32),
        shares[4],
        shares[5],
        shares[6],
        up_grad.astype(f32),
        shares[8],
        down_grad.T.astype(f32),
        shares[7],
    )


def solution(mesh):
    rows = P(BOTH, None, None)
    vector = P(BOTH)
    return jax.shard_map(
        shards,
        mesh=mesh,
        in_specs=(
            rows,
            P("dp"),
            rows,
            vector,
            vector,
            P(None, "dp", "tensor"),
            vector,
            vector,
            P("tensor", "dp"),
            vector,
            vector,
            vector,
            P("dp", "tensor"),
            vector,
            P("tensor", "dp"),
            vector,
        ),
        out_specs=(
            rows,
            rows,
            vector,
            vector,
            P(None, "dp", "tensor"),
            vector,
            vector,
            P("tensor", "dp"),
            vector,
            vector,
            vector,
            P("dp", "tensor"),
            vector,
            P("tensor", "dp"),
            vector,
        ),
        check_vma=False,
    )
```

profile of v0, /device:TPU:0, one launch (start us, length us, event | category | flops | bytes accessed | tf_op | source)
XLA Modules:
  0.0 1265.5 jit_solution(6776043386296748097)
XLA Ops:
  8.4 6.0 all-gather.5
  14.5 5.0 all-gather.1
  19.6 5.0 all-gather.3
  24.7 7.3 all_gather.50
  32.1 9.3 all_gather.52
  41.5 7.3 all_gather.54
  50.6 65.8 %all-gather.7 = bf16[32,1,384]{2,1,0:T(2,128)(2,1)S(1)} all-gather(bf16[1,1,384]{2,1,0:T(2,128)(2,1)S(1)} %reshape.425), channel_id=2, replica_groups=mesh['dp'=16,'tensor'=2] {'dp','tensor'}, dimensions={0}, use_global_device_ids=true | all-gather | bytes 25344 | tf_op jit(solution)/shard_map/all_gather | solution.py:89
  133.1 5.2 add_convert_fusion.5
  161.5 11.1 fusion.63
  172.6 7.6 fusion.45
  190.6 69.1 %all-gather.17.cloned.1.call-done = bf16[1024,4096]{1,0:T(8,128)(2,1)} async-done(((bf16[64,4096]{1,0:T(8,128)(2,1)}), bf16[1024,4096]{1,0:T(8,128)(2,1)}) %all-gather.17.cloned.1.call-update) | async-done | bytes 8388624 | tf_op jit(solution)/shard_map/all_gather | solution.py:34
  259.7 11.4 fusion.60
  271.1 63.5 %all-gather.19.cloned.1.call-done = bf16[1024,4096]{1,0:T(8,128)(2,1)} async-done(((bf16[64,4096]{1,0:T(8,128)(2,1)}), bf16[1024,4096]{1,0:T(8,128)(2,1)}) %all-gather.19.cloned.1.call-update) | async-done | bytes 8388624 | tf_op jit(solution)/shard_map/all_gather | solution.py:34
  334.7 35.0 %convert_reduce_fusion = (f32[4096]{0:T(1024)}, bf16[640,4096]{1,0:T(8,128)(2,1)S(1)}, f32[640,4096]{1,0:T(8,128)}) fusion(f32[640,4096]{1,0:T(8,128)} %fusion.60, f32[4096]{0:T(1024)S(1)} %fusion.54, bf16[640,1024]{1,0:T(8,128)(2,1)} %bitcast.173, bf16[1024,4096]{1,0:T(8,128)(2,1)} %all-gather.19.cloned.1.call-done), kind=kOutput, calls=%fused_computation.8 | convolution fusion | flops 5565313024 | bytes 35946496 | tf_op jit(solution)/shard_map/dot_general | solution.py:45
  369.7 6.1 multiply_reduce_fusion.1
  385.6 5.0 copy.72
  390.5 8.6 convert_reduce_fusion.1
  411.8 14.3 %multiply_reduce_fusion = (f32[2,16,320]{2,1,0:T(8,128)S(1)}, f32[2,16,320,320]{2,3,1,0:T(8,128)}) fusion(f32[2,16,320,320]{2,3,1,0:T(8,128)} %get-tuple-element.62, f32[2,16,320]{2,1,0:T(8,128)S(1)} %get-tuple-element.61, bf16[2,320,16,64]{1,3,2,0:T(8,128)(2,1)} %copy.72, bf16[2,320,16,64]{1,3,2,0:T(8,128)(2,1)} %copy.68), kind=kOutput, calls=%fused_computation.2 | convolution fusion | flops 429250560 | bytes 28917760 | tf_op jit(solution)/shard_map/bqhc,bkhc->bhqk/dot_general | solution.py:142
  426.1 11.2 multiply_convert_fusion
  453.0 5.4 convert_reduce_fusion.2
  477.3 9.7 convolution_convert_fusion
  489.4 6.2 pad_maximum_fusion
  495.7 8.2 multiply_convert_fusion.1
  504.0 7.3 convert_bitcast_fusion
  513.7 6.2 pad_maximum_fusion.1
  531.4 39.9 %all-reduce = f32[32,384]{1,0:T(8,128)S(1)} all-reduce(f32[32,384]{1,0:T(8,128)S(1)} %concatenate.7), channel_id=9, replica_groups=mesh['dp'=16,'tensor'=2] {'dp','tensor'}, use_global_device_ids=true, to_apply=%region_20.21.clone | all-reduce | flops 12288 | bytes 98304
  576.8 10.5 add_convert_fusion.2
  587.3 98.5 %reduce-scatter.9.cloned.1.call-done = bf16[64,512]{1,0:T(8,128)(2,1)} async-done(((bf16[2048,512]{1,0:T(8,128)(2,1)}), bf16[64,512]{1,0:T(8,128)(2,1)}) %reduce-scatter.9.cloned.1.call-update) | async-done | bytes 65552 | tf_op jit(solution)/shard_map/reduce_scatter | solution.py:41
  685.8 136.7 %reduce-scatter.7.cloned.1.call-done = bf16[64,512]{1,0:T(8,128)(2,1)} async-done(((bf16[2048,512]{1,0:T(8,128)(2,1)}), bf16[64,512]{1,0:T(8,128)(2,1)}) %reduce-scatter.7.cloned.1.call-update) | async-done | bytes 65552 | tf_op jit(solution)/shard_map/reduce_scatter | solution.py:41
  824.2 134.9 %reduce-scatter.13.cloned.1.call-done = bf16[64,512]{1,0:T(8,128)(2,1)} async-done(((bf16[2048,512]{1,0:T(8,128)(2,1)}), bf16[64,512]{1,0:T(8,128)(2,1)}) %reduce-scatter.13.cloned.1.call-update) | async-done | bytes 65552 | tf_op jit(solution)/shard_map/reduce_scatter | solution.py:41
  960.6 147.0 %reduce-scatter.15.cloned.1.call-done = bf16[64,2048]{1,0:T(8,128)(2,1)} async-done(((bf16[2048,2048]{1,0:T(8,128)(2,1)}), bf16[64,2048]{1,0:T(8,128)(2,1)}) %reduce-scatter.15.cloned.1.call-update) | async-done | bytes 262160 | tf_op jit(solution)/shard_map/reduce_scatter | solution.py:41
  1109.4 147.2 %reduce-scatter.17.cloned.1.call-done = bf16[64,2048]{1,0:T(8,128)(2,1)} async-done(((bf16[2048,2048]{1,0:T(8,128)(2,1)}), bf16[64,2048]{1,0:T(8,128)(2,1)}) %reduce-scatter.17.cloned.1.call-update) | async-done | bytes 262160 | tf_op jit(solution)/shard_map/reduce_scatter | solution.py:41
  (201 shorter events, 138.5 us)
Async XLA Ops:
  7.2 34.3 %copy-start.15 = (bf16[2048,64]{0,1:T(8,128)(2,1)S(1)}, bf16[2048,64]{0,1:T(8,128)(2,1)}, u32[]{:S(2)}) copy-start(bf16[2048,64]{0,1:T(8,128)(2,1)} %param.30) | copy-start | bytes 786436
  7.2 41.8 %copy-start.35 = (bf16[32]{0:T(256)(128)(2,1)S(1)}, bf16[32]{0:T(256)(128)(2,1)}, u32[]{:S(2)}) copy-start(bf16[32]{0:T(256)(128)(2,1)} %param.31) | copy-start | bytes 196
  7.2 41.8 %copy-start.36 = (bf16[128]{0:T(256)(128)(2,1)S(1)}, bf16[128]{0:T(256)(128)(2,1)}, u32[]{:S(2)}) copy-start(bf16[128]{0:T(256)(128)(2,1)} %param.29) | copy-start | bytes 772
  7.2 41.8 %copy-start.34 = (bf16[32]{0:T(256)(128)(2,1)S(1)}, bf16[32]{0:T(256)(128)(2,1)}, u32[]{:S(2)}) copy-start(bf16[32]{0:T(256)(128)(2,1)} %param.27) | copy-start | bytes 196
  7.2 41.8 %copy-start.33 = (bf16[32]{0:T(256)(128)(2,1)S(1)}, bf16[32]{0:T(256)(128)(2,1)}, u32[]{:S(2)}) copy-start(bf16[32]{0:T(256)(128)(2,1)} %param.26) | copy-start | bytes 196
  7.2 41.8 %copy-start.32 = (bf16[32]{0:T(256)(128)(2,1)S(1)}, bf16[32]{0:T(256)(128)(2,1)}, u32[]{:S(2)}) copy-start(bf16[32]{0:T(256)(128)(2,1)} %param.25) | copy-start | bytes 196
  7.2 41.8 %copy-start.31 = (bf16[32]{0:T(256)(128)(2,1)S(1)}, bf16[32]{0:T(256)(128)(2,1)}, u32[]{:S(2)}) copy-start(bf16[32]{0:T(256)(128)(2,1)} %param.23) | copy-start | bytes 196
  7.3 41.8 %copy-start.30 = (bf16[32]{0:T(256)(128)(2,1)S(1)}, bf16[32]{0:T(256)(128)(2,1)}, u32[]{:S(2)}) copy-start(bf16[32]{0:T(256)(128)(2,1)} %param.22) | copy-start | bytes 196
  7.3 41.8 %copy-start.29 = (bf16[32]{0:T(256)(128)(2,1)S(1)}, bf16[32]{0:T(256)(128)(2,1)}, u32[]{:S(2)}) copy-start(bf16[32]{0:T(256)(128)(2,1)} %param.20) | copy-start | bytes 196
  7.3 41.8 %copy-start.28 = (bf16[32]{0:T(256)(128)(2,1)S(1)}, bf16[32]{0:T(256)(128)(2,1)}, u32[]{:S(2)}) copy-start(bf16[32]{0:T(256)(128)(2,1)} %param.19) | copy-start | bytes 196
  7.3 41.9 %copy-start.41 = (s32[4]{0:T(128)S(1)}, s32[4]{0:T(128)}, u32[]{:S(2)}) copy-start(s32[4]{0:T(128)} %param.17) | copy-start | bytes 52
  7.3 42.1 %copy-start.1 = (bf16[2,320,1024]{2,1,0:T(8,128)(2,1)S(1)}, bf16[2,320,1024]{2,1,0:T(8,128)(2,1)}, u32[]{:S(2)}) copy-start(bf16[2,320,1024]{2,1,0:T(8,128)(2,1)} %param.16) | copy-start | bytes 3932164
  7.3 112.7 %all-gather.25.cloned.1.call-start = ((), (), s32[]{:S(2)}) async-start(), calls=%async_computation.17 | async-start | bytes 2228224 | tf_op jit(solution)/shard_map/all_gather | solution.py:34
  14.4 118.7 %all-gather.21.cloned.1.call-start = ((), (), s32[]{:S(2)}) async-start(), calls=%async_computation.15 | async-start | bytes 2228224 | tf_op jit(solution)/shard_map/all_gather | solution.py:34
  19.5 128.0 %all-gather.23.cloned.1.call-start = ((), (), s32[]{:S(2)}) async-start(), calls=%async_computation.16 | async-start | bytes 2228224 | tf_op jit(solution)/shard_map/all_gather | solution.py:34
  24.7 160.0 %all-gather.15.cloned.1.call-start = ((), (), s32[]{:S(2)}) async-start(), calls=%async_computation.6 | async-start | bytes 2228224 | tf_op jit(solution)/shard_map/all_gather | solution.py:34
  32.1 227.6 %all-gather.17.cloned.1.call-start = ((), (), s32[]{:S(2)}) async-start(), calls=%async_computation.7 | async-start | bytes 8912896 | tf_op jit(solution)/shard_map/all_gather | solution.py:34
  41.5 293.2 %all-gather.19.cloned.1.call-start = ((), (), s32[]{:S(2)}) async-start(), calls=%async_computation.8 | async-start | bytes 8912896 | tf_op jit(solution)/shard_map/all_gather | solution.py:34
  48.9 538.4 %reduce-scatter.11.cloned.1.call-start = ((), (), s32[]{:S(2)}) async-start(), calls=%async_computation.11 | async-start | bytes 2162688 | tf_op jit(solution)/shard_map/reduce_scatter | solution.py:41
  49.4 135.3 %copy-start.19 = (f32[640]{0:T(1024)}, f32[640]{0:T(1024)S(1)}, u32[]{:S(2)}) copy-start(f32[640]{0:T(1024)S(1)} %reshape.408) | copy-start | bytes 7684
  49.9 70.0 %copy-start.21 = (f32[640]{0:T(1024)}, f32[640]{0:T(1024)S(1)}, u32[]{:S(2)}) copy-start(f32[640]{0:T(1024)S(1)} %div.35) | copy-start | bytes 7684
  50.6 69.4 %copy-start.23 = (f32[640]{0:T(1024)}, f32[640]{0:T(1024)S(1)}, u32[]{:S(2)}) copy-start(f32[640]{0:T(1024)S(1)} %rsqrt.21) | copy-start | bytes 7684
  117.3 142.4 %copy-start.26 = (f32[1024]{0:T(1024)}, f32[1024]{0:T(1024)S(1)}, u32[]{:S(2)}) copy-start(f32[1024]{0:T(1024)S(1)} %reshape.415) | copy-start | bytes 12292
  133.1 28.4 %copy-start.7 = (bf16[2,320,16,64]{1,3,2,0:T(8,128)(2,1)}, bf16[2,320,16,64]{1,3,2,0:T(8,128)(2,1)S(1)}, u32[]{:S(2)}) copy-start(bf16[2,320,16,64]{1,3,2,0:T(8,128)(2,1)S(1)} %copy.67) | copy-start | bytes 3932164
  334.6 35.0 %copy-start.4 = (f32[640,1024]{1,0:T(8,128)S(1)}, f32[640,1024]{1,0:T(8,128)}, u32[]{:S(2)}) copy-start(f32[640,1024]{1,0:T(8,128)} %copy-done.3) | copy-start | bytes 7864324
  334.7 35.0 %copy-start.37 = (bf16[1024,4096]{1,0:T(8,128)(2,1)S(1)}, bf16[1024,4096]{1,0:T(8,128)(2,1)}, u32[]{:S(2)}) copy-start(bf16[1024,4096]{1,0:T(8,128)(2,1)} %all-gather.17.cloned.1.call-done) | copy-start | bytes 25165828
  411.7 274.1 %reduce-scatter.9.cloned.1.call-start = ((), (), s32[]{:S(2)}) async-start(), calls=%async_computation.10 | async-start | bytes 2162688 | tf_op jit(solution)/shard_map/reduce_scatter | solution.py:41
  426.1 11.2 copy-start.8
  453.0 369.6 %reduce-scatter.7.cloned.1.call-start = ((), (), s32[]{:S(2)}) async-start(), calls=%async_computation.9 | async-start | bytes 2162688 | tf_op jit(solution)/shard_map/reduce_scatter | solution.py:41
  471.4 487.7 %reduce-scatter.13.cloned.1.call-start = ((), (), s32[]{:S(2)}) async-start(), calls=%async_computation.12 | async-start | bytes 2162688 | tf_op jit(solution)/shard_map/reduce_scatter | solution.py:41
  477.2 630.4 %reduce-scatter.15.cloned.1.call-start = ((), (), s32[]{:S(2)}) async-start(), calls=%async_computation.13 | async-start | bytes 8650752 | tf_op jit(solution)/shard_map/reduce_scatter | solution.py:41
  495.7 761.0 %reduce-scatter.17.cloned.1.call-start = ((), (), s32[]{:S(2)}) async-start(), calls=%async_computation.14 | async-start | bytes 8650752 | tf_op jit(solution)/shard_map/reduce_scatter | solution.py:41
  (23 other events, 74.7 us)
Sparse Core Ops, SparseCore 0:
  14.5 43.2 all-gather.24
  60.0 40.1 all-gather.20
  102.4 40.0 all-gather.22
  144.5 40.1 all-gather.14
  186.7 73.0 all-gather.16
  261.7 72.8 all-gather.18
  411.9 137.0 reduce-scatter.10
  551.3 134.4 reduce-scatter.8
  688.1 134.4 reduce-scatter.6
  824.6 134.4 reduce-scatter.12
  961.4 146.1 reduce-scatter.14
  1109.8 146.8 reduce-scatter.16
where the time goes:
time: 1270 us
  waiting for transfers between devices  798 us (63%)
  matrix products  174 us (14%)
  blocking collectives  146 us (11%)
  local copies, waits for them, and re-layouts  76.5 us (6%)
  other arithmetic  55 us (4%)
  between operations  15.2 us (1%)
    reduce_scatter x6, waiting for transfers between devices, scatter_matrix(): lax.psum_scatter(halves, ('tensor', 'dp'), scatter_dimension=0, tiled=True)  664 us
    all_gather x6, waiting for transfers between devices, gather_matrix(): return lax.all_gather(wide, 'dp', axis=0, tiled=True)  134 us
    dot_general x18, matrix products, mm(): return lax.dot_general(a, b, (dims, ((), ())), preferred_element_type=f32)  125 us
    all_gather x1, blocking collectives, shards(): packed = lax.all_gather(jnp.concatenate(vectors), BOTH, axis=0)  65.8 us
    all_gather x6, blocking collectives, gather_matrix(): wide = lax.all_gather(shard, 'tensor', axis=1, tiled=True)  40.1 us
    unnamed x1, blocking collectives  39.9 us
    reshape x8, local copies, waits for them, and re-layouts, split(): return rows.reshape(image_count, slot_count, heads, HEAD_DIM)  36.3 us
  transfers between devices with their start and end apart: 12, of which 8 were waited for; matrix products, arithmetic and copies ran while one was open for 18% of the time, Pallas kernels for 0%

commit v1 on v0

--- a/solution.py
+++ b/solution.py
@@ -8,6 +8,28 @@
 BOTH = ("dp", "tensor")
 bf16 = jnp.bfloat16
 f32 = jnp.float32
+
+
+def in_order(tiles, dim):
+    tiles = jnp.moveaxis(tiles, 0, dim)
+    lengths = tiles.shape
+    return tiles.reshape(*lengths[:dim], lengths[dim] * lengths[dim + 1], *lengths[dim + 2 :])
+
+
+def doubled(array, axis):
+    size = lax.axis_size(axis)
+    blocks = array[None]
+    for level in range(size.bit_length() - 1):
+        apart = 1 << level
+        theirs = lax.ppermute(blocks, axis, [(i, i ^ apart) for i in range(size)])
+        both = jnp.stack([blocks, theirs])
+        upper = lax.axis_index(axis) >> level & 1
+        blocks = jnp.where(upper == 0, both, both[::-1]).reshape(-1, *array.shape)
+    return blocks
+
+
+def doubled_up(x, axis, dim):
+    return in_order(doubled(x, axis), dim)
 
 
 def exact_gelu(values):
@@ -31,7 +53,7 @@
 
 def gather_matrix(shard):
     wide = lax.all_gather(shard, "tensor", axis=1, tiled=True)
-    return lax.all_gather(wide, "dp", axis=0, tiled=True)
+    return doubled_up(wide, "dp", 0)
 
 
 def scatter_matrix(grad):

time: 1270 us -> 1780 us (1.40)
  waiting for transfers between devices: 798 us -> 1220 us
  other arithmetic: 55 us -> 118 us
    ppermute x0 -> x24, waiting for transfers between devices: none -> 543 us  [doubled(): theirs = lax.ppermute(blocks, axis, [(i, i ^ apart) for i in range(size)])]
    all_gather x6 -> x0, waiting for transfers between devices: 134 us -> none  [gather_matrix(): return lax.all_gather(wide, 'dp', axis=0, tiled=True)]
    select_n x0 -> x18, other arithmetic: none -> 43.6 us  [doubled(): blocks = jnp.where(upper == 0, both, both[::-1]).reshape(-1, *array.shape)]
    another operation x0 -> x30, other arithmetic: none -> 28 us  [doubled(): both = jnp.stack([blocks, theirs])]
  transfers between devices with their start and end apart: 12 -> 30, of which waited for: 8 -> 14; matrix products, arithmetic and copies ran while one was open for 18% -> 14% of each run, Pallas kernels for 0% -> 0%
where the time goes in v1:
time: 1780 us; the launch traced here: 1770 us
  waiting for transfers between devices  1220 us (69%)
  matrix products  170 us (10%)
  blocking collectives  146 us (8%)
  other arithmetic  118 us (7%)
  local copies, waits for them, and re-layouts  84.4 us (5%)
  starting transfers between devices  18 us (1%)
    reduce_scatter x6, waiting for transfers between devices, scatter_matrix(): lax.psum_scatter(halves, ('tensor', 'dp'), scatter_dimension=0, tiled=True)  680 us
    ppermute x24, waiting for transfers between devices, doubled(): theirs = lax.ppermute(blocks, axis, [(i, i ^ apart) for i in range(size)])  543 us
    dot_general x18, matrix products, mm(): return lax.dot_general(a, b, (dims, ((), ())), preferred_element_type=f32)  128 us
    all_gather x1, blocking collectives, shards(): packed = lax.all_gather(jnp.concatenate(vectors), BOTH, axis=0)  69.3 us
    select_n x18, other arithmetic, doubled(): blocks = jnp.where(upper == 0, both, both[::-1]).reshape(-1, *array.shape)  43.6 us
    all_gather x6, blocking collectives, gather_matrix(): wide = lax.all_gather(shard, 'tensor', axis=1, tiled=True)  38.7 us
    unnamed x1, blocking collectives  37.6 us
    reshape x8, local copies, waits for them, and re-layouts, split(): return rows.reshape(image_count, slot_count, heads, HEAD_DIM)  36.8 us
  transfers between devices with their start and end apart: 30, of which 14 were waited for; matrix products, arithmetic and copies ran while one was open for 14% of the time, Pallas kernels for 0%

profile of v1, /device:TPU:0, one launch (start us, length us, event | category | flops | bytes accessed | tf_op | source)
XLA Modules:
  0.0 1774.7 jit_solution(11829527573890441382)
XLA Ops:
  7.2 6.3 all_gather.29
  30.2 9.6 all_gather.31
  45.9 69.3 %all-gather.4 = bf16[32,1,384]{2,1,0:T(2,128)(2,1)S(1)} all-gather(bf16[1,1,384]{2,1,0:T(2,128)(2,1)S(1)} %reshape.578), channel_id=2, replica_groups=mesh['dp'=16,'tensor'=2] {'dp','tensor'}, dimensions={0}, use_global_device_ids=true | all-gather | bytes 25344 | tf_op jit(solution)/shard_map/all_gather | solution.py:111
  130.0 7.0 all_gather.30
  140.6 17.5 collective-permute-done.9
  158.5 7.4 collective-permute-done.1
  172.1 31.2 %collective-permute-done.6 = bf16[4,64,1024]{2,1,0:T(8,128)(2,1)S(1)} collective-permute-done((bf16[4,64,1024]{2,1,0:T(8,128)(2,1)S(1)}, bf16[4,64,1024]{2,1,0:T(8,128)(2,1)S(1)}, u32[]{:S(2)}, u32[]{:S(2)}) %collective-permute-start.6) | collective-permute-done | bytes 524320 | tf_op jit(solution)/shard_map/ppermute | solution.py:24
  203.9 8.4 collective-permute-done.14
  225.5 125.0 %collective-permute-done.7 = bf16[8,64,1024]{2,1,0:T(8,128)(2,1)S(1)} collective-permute-done((bf16[8,64,1024]{2,1,0:T(8,128)(2,1)S(1)}, bf16[8,64,1024]{2,1,0:T(8,128)(2,1)S(1)}, u32[]{:S(2)}, u32[]{:S(2)}) %collective-permute-start.7) | collective-permute-done | bytes 1048608 | tf_op jit(solution)/shard_map/ppermute | solution.py:24
  364.8 30.8 %collective-permute-done.11 = bf16[8,64,1024]{2,1,0:T(8,128)(2,1)} collective-permute-done((bf16[8,64,1024]{2,1,0:T(8,128)(2,1)}, bf16[8,64,1024]{2,1,0:T(8,128)(2,1)}, u32[]{:S(2)}, u32[]{:S(2)}) %collective-permute-start.11) | collective-permute-done | bytes 1048608 | tf_op jit(solution)/shard_map/ppermute | solution.py:24
  414.7 11.1 fusion.61
  465.0 253.7 %collective-permute-done.23 = bf16[8,64,4096]{2,1,0:T(8,128)(2,1)} collective-permute-done((bf16[8,64,4096]{2,1,0:T(8,128)(2,1)}, bf16[8,64,4096]{2,1,0:T(8,128)(2,1)}, u32[]{:S(2)}, u32[]{:S(2)}) %collective-permute-start.23) | collective-permute-done | bytes 4194336 | tf_op jit(solution)/shard_map/ppermute | solution.py:24
  718.6 7.4 pad_maximum_fusion.1
  726.1 13.5 reverse_select_fusion
  739.5 68.9 %collective-permute-done.19 = bf16[8,64,4096]{2,1,0:T(8,128)(2,1)} collective-permute-done((bf16[8,64,4096]{2,1,0:T(8,128)(2,1)}, bf16[8,64,4096]{2,1,0:T(8,128)(2,1)}, u32[]{:S(2)}, u32[]{:S(2)}) %collective-permute-start.19) | collective-permute-done | bytes 4194336 | tf_op jit(solution)/shard_map/ppermute | solution.py:24
  808.4 7.4 pad_maximum_fusion
  815.9 13.7 reverse_select_fusion.1
  829.6 33.5 %multiply_convert_fusion.1 = (bf16[640,4096]{1,0:T(8,128)(2,1)}, f32[640,4096]{1,0:T(8,128)}, f32[640,4096]{1,0:T(8,128)}) fusion(f32[4096]{0:T(1024)S(1)} %copy-done.35, bf16[1024,4096]{1,0:T(8,128)(2,1)} %bitcast.278, f32[640,1024]{1,0:T(8,128)S(1)} %get-tuple-element.75, f32[1024]{0:T(1024)S(1)} %copy-done.36, f32[1024]{0:T(1024)S(1)} %copy-done.31, ...), kind=kOutput, calls=%fused_computation.20 | convolution fusion | flops 5545000960 | bytes 37254144 | tf_op jit(solution)/shard_map/dot_general | solution.py:67
  863.1 16.3 convert_reduce_fusion
  879.4 10.7 multiply_reduce_fusion.1
  903.8 8.6 convert_reduce_fusion.1
  922.0 13.8 multiply_reduce_fusion
  935.9 11.0 multiply_convert_fusion
  978.8 10.0 convolution_convert_fusion
  997.9 9.5 convert_bitcast_fusion
  1027.2 37.6 %all-reduce = f32[32,384]{1,0:T(8,128)S(1)} all-reduce(f32[32,384]{1,0:T(8,128)S(1)} %concatenate.7), channel_id=6, replica_groups=mesh['dp'=16,'tensor'=2] {'dp','tensor'}, use_global_device_ids=true, to_apply=%region_20.21.clone | all-reduce | flops 12288 | bytes 98304
  1070.4 10.5 add_convert_fusion
  1080.8 114.0 %reduce-scatter.9.cloned.1.call-done = bf16[64,512]{1,0:T(8,128)(2,1)} async-done(((bf16[2048,512]{1,0:T(8,128)(2,1)}), bf16[64,512]{1,0:T(8,128)(2,1)}) %reduce-scatter.9.cloned.1.call-update) | async-done | bytes 65552 | tf_op jit(solution)/shard_map/reduce_scatter | solution.py:63
  1194.8 137.1 %reduce-scatter.7.cloned.1.call-done = bf16[64,512]{1,0:T(8,128)(2,1)} async-done(((bf16[2048,512]{1,0:T(8,128)(2,1)}), bf16[64,512]{1,0:T(8,128)(2,1)}) %reduce-scatter.7.cloned.1.call-update) | async-done | bytes 65552 | tf_op jit(solution)/shard_map/reduce_scatter | solution.py:63
  1333.6 135.4 %reduce-scatter.13.cloned.1.call-done = bf16[64,512]{1,0:T(8,128)(2,1)} async-done(((bf16[2048,512]{1,0:T(8,128)(2,1)}), bf16[64,512]{1,0:T(8,128)(2,1)}) %reduce-scatter.13.cloned.1.call-update) | async-done | bytes 65552 | tf_op jit(solution)/shard_map/reduce_scatter | solution.py:63
  1470.5 146.9 %reduce-scatter.15.cloned.1.call-done = bf16[64,2048]{1,0:T(8,128)(2,1)} async-done(((bf16[2048,2048]{1,0:T(8,128)(2,1)}), bf16[64,2048]{1,0:T(8,128)(2,1)}) %reduce-scatter.15.cloned.1.call-update) | async-done | bytes 262160 | tf_op jit(solution)/shard_map/reduce_scatter | solution.py:63
  1619.2 146.7 %reduce-scatter.17.cloned.1.call-done = bf16[64,2048]{1,0:T(8,128)(2,1)} async-done(((bf16[2048,2048]{1,0:T(8,128)(2,1)}), bf16[64,2048]{1,0:T(8,128)(2,1)}) %reduce-scatter.17.cloned.1.call-update) | async-done | bytes 262160 | tf_op jit(solution)/shard_map/reduce_scatter | solution.py:63
  (284 shorter events, 229.7 us)
Async XLA Ops:
  7.2 1073.7 %reduce-scatter.11.cloned.1.call-start = ((), (), s32[]{:S(2)}) async-start(), calls=%async_computation.8 | async-start | bytes 2162688 | tf_op jit(solution)/shard_map/reduce_scatter | solution.py:63
  13.5 123.5 %collective-permute-start.12 = (bf16[1,64,1024]{2,1,0:T(8,128)(2,1)S(1)}, bf16[1,64,1024]{2,1,0:T(8,128)(2,1)}, u32[]{:S(2)}, u32[]{:S(2)}) collective-permute-start(bf16[1,64,1024]{2,1,0:T(8,128)(2,1)S(1)} %bitcast.323), channel_id=1, source_target_pairs={{0,2},{2,0},{4,6},{6,4},{8,10},{10,8},{12,14},{14,12},{16,18},{18,... | collective-permute-start | bytes 393224 | tf_op jit(solution)/shard_map/ppermute | solution.py:24
  19.9 118.2 %collective-permute-start.4 = (bf16[1,64,1024]{2,1,0:T(8,128)(2,1)S(1)}, bf16[1,64,1024]{2,1,0:T(8,128)(2,1)S(1)}, u32[]{:S(2)}, u32[]{:S(2)}) collective-permute-start(bf16[1,64,1024]{2,1,0:T(8,128)(2,1)S(1)} %all-gather.2), channel_id=1, source_target_pairs={{0,2},{2,0},{4,6},{6,4},{8,10},{10,8},{12,14},{14,12},{16,18},{18,... | collective-permute-start | bytes 393224 | tf_op jit(solution)/shard_map/ppermute | solution.py:24
  25.0 115.4 %collective-permute-start = (bf16[1,64,1024]{2,1,0:T(8,128)(2,1)S(1)}, bf16[1,64,1024]{2,1,0:T(8,128)(2,1)S(1)}, u32[]{:S(2)}, u32[]{:S(2)}) collective-permute-start(bf16[1,64,1024]{2,1,0:T(8,128)(2,1)S(1)} %all-gather.1), channel_id=1, source_target_pairs={{0,2},{2,0},{4,6},{6,4},{8,10},{10,8},{12,14},{14,12},{16,18},{18,... | collective-permute-start | bytes 393224 | tf_op jit(solution)/shard_map/ppermute | solution.py:24
  30.2 108.1 %collective-permute-start.8 = (bf16[1,64,1024]{2,1,0:T(8,128)(2,1)S(1)}, bf16[1,64,1024]{2,1,0:T(8,128)(2,1)S(1)}, u32[]{:S(2)}, u32[]{:S(2)}) collective-permute-start(bf16[1,64,1024]{2,1,0:T(8,128)(2,1)S(1)} %all-gather.3), channel_id=1, source_target_pairs={{0,2},{2,0},{4,6},{6,4},{8,10},{10,8},{12,14},{14,12},{16,18},{18,... | collective-permute-start | bytes 393224 | tf_op jit(solution)/shard_map/ppermute | solution.py:24
  39.8 131.3 %collective-permute-start.20 = (bf16[1,64,4096]{2,1,0:T(8,128)(2,1)S(1)}, bf16[1,64,4096]{2,1,0:T(8,128)(2,1)S(1)}, u32[]{:S(2)}, u32[]{:S(2)}) collective-permute-start(bf16[1,64,4096]{2,1,0:T(8,128)(2,1)S(1)} %bitcast.299), channel_id=1, source_target_pairs={{0,2},{2,0},{4,6},{6,4},{8,10},{10,8},{12,14},{14,12},{16,18},{18,... | collective-permute-start | bytes 1572872 | tf_op jit(solution)/shard_map/ppermute | solution.py:24
  130.0 221.3 %copy-start.17 = (bf16[2,320,1024]{2,1,0:T(8,128)(2,1)}, bf16[2,320,1024]{2,1,0:T(8,128)(2,1)S(1)}, u32[]{:S(2)}) copy-start(bf16[2,320,1024]{2,1,0:T(8,128)(2,1)S(1)} %add_convert_fusion.4) | copy-start | bytes 3932164
  137.1 31.6 %collective-permute-start.16 = (bf16[1,64,4096]{2,1,0:T(8,128)(2,1)S(1)}, bf16[1,64,4096]{2,1,0:T(8,128)(2,1)S(1)}, u32[]{:S(2)}, u32[]{:S(2)}) collective-permute-start(bf16[1,64,4096]{2,1,0:T(8,128)(2,1)S(1)} %bitcast.301), channel_id=1, source_target_pairs={{0,2},{2,0},{4,6},{6,4},{8,10},{10,8},{12,14},{14,12},{16,18},{18,... | collective-permute-start | bytes 1572872 | tf_op jit(solution)/shard_map/ppermute | solution.py:24
  138.1 30.3 %collective-permute-start.13 = (bf16[2,64,1024]{2,1,0:T(8,128)(2,1)S(1)}, bf16[2,64,1024]{2,1,0:T(8,128)(2,1)S(1)}, u32[]{:S(2)}, u32[]{:S(2)}) collective-permute-start(bf16[2,64,1024]{2,1,0:T(8,128)(2,1)S(1)} %get-tuple-element.44), channel_id=1, source_target_pairs={{0,4},{2,6},{4,0},{6,2},{8,12},{10,14},{12,8},{14,10},{16,20},{18,... | collective-permute-start | bytes 786440 | tf_op jit(solution)/shard_map/ppermute | solution.py:24
  138.3 27.9 %collective-permute-start.5 = (bf16[2,64,1024]{2,1,0:T(8,128)(2,1)S(1)}, bf16[2,64,1024]{2,1,0:T(8,128)(2,1)S(1)}, u32[]{:S(2)}, u32[]{:S(2)}) collective-permute-start(bf16[2,64,1024]{2,1,0:T(8,128)(2,1)S(1)} %get-tuple-element.48), channel_id=1, source_target_pairs={{0,4},{2,6},{4,0},{6,2},{8,12},{10,14},{12,8},{14,10},{16,20},{18,... | collective-permute-start | bytes 786440 | tf_op jit(solution)/shard_map/ppermute | solution.py:24
  140.5 17.6 collective-permute-start.9
  158.1 7.9 collective-permute-start.1
  165.9 52.2 %collective-permute-start.10 = (bf16[4,64,1024]{2,1,0:T(8,128)(2,1)S(1)}, bf16[4,64,1024]{2,1,0:T(8,128)(2,1)S(1)}, u32[]{:S(2)}, u32[]{:S(2)}) collective-permute-start(bf16[4,64,1024]{2,1,0:T(8,128)(2,1)S(1)} %bitcast.303), channel_id=1, source_target_pairs={{0,8},{2,10},{4,12},{6,14},{8,0},{10,2},{12,4},{14,6},{16,24},{18,... | collective-permute-start | bytes 1572872 | tf_op jit(solution)/shard_map/ppermute | solution.py:24
  166.1 47.8 %collective-permute-start.2 = (bf16[4,64,1024]{2,1,0:T(8,128)(2,1)S(1)}, bf16[4,64,1024]{2,1,0:T(8,128)(2,1)S(1)}, u32[]{:S(2)}, u32[]{:S(2)}) collective-permute-start(bf16[4,64,1024]{2,1,0:T(8,128)(2,1)S(1)} %bitcast.305), channel_id=1, source_target_pairs={{0,8},{2,10},{4,12},{6,14},{8,0},{10,2},{12,4},{14,6},{16,24},{18,... | collective-permute-start | bytes 1572872 | tf_op jit(solution)/shard_map/ppermute | solution.py:24
  168.4 34.8 %collective-permute-start.6 = (bf16[4,64,1024]{2,1,0:T(8,128)(2,1)S(1)}, bf16[4,64,1024]{2,1,0:T(8,128)(2,1)S(1)}, u32[]{:S(2)}, u32[]{:S(2)}) collective-permute-start(bf16[4,64,1024]{2,1,0:T(8,128)(2,1)S(1)} %bitcast.307), channel_id=1, source_target_pairs={{0,8},{2,10},{4,12},{6,14},{8,0},{10,2},{12,4},{14,6},{16,24},{18,... | collective-permute-start | bytes 1572872 | tf_op jit(solution)/shard_map/ppermute | solution.py:24
  168.7 43.6 %collective-permute-start.14 = (bf16[4,64,1024]{2,1,0:T(8,128)(2,1)S(1)}, bf16[4,64,1024]{2,1,0:T(8,128)(2,1)S(1)}, u32[]{:S(2)}, u32[]{:S(2)}) collective-permute-start(bf16[4,64,1024]{2,1,0:T(8,128)(2,1)S(1)} %bitcast.309), channel_id=1, source_target_pairs={{0,8},{2,10},{4,12},{6,14},{8,0},{10,2},{12,4},{14,6},{16,24},{18,... | collective-permute-start | bytes 1572872 | tf_op jit(solution)/shard_map/ppermute | solution.py:24
  171.4 48.1 %collective-permute-start.21 = (bf16[2,64,4096]{2,1,0:T(8,128)(2,1)S(1)}, bf16[2,64,4096]{2,1,0:T(8,128)(2,1)S(1)}, u32[]{:S(2)}, u32[]{:S(2)}) collective-permute-start(bf16[2,64,4096]{2,1,0:T(8,128)(2,1)S(1)} %get-tuple-element.40), channel_id=1, source_target_pairs={{0,4},{2,6},{4,0},{6,2},{8,12},{10,14},{12,8},{14,10},{16,20},{18,... | collective-permute-start | bytes 3145736 | tf_op jit(solution)/shard_map/ppermute | solution.py:24
  203.2 21.2 %collective-permute-start.17 = (bf16[2,64,4096]{2,1,0:T(8,128)(2,1)S(1)}, bf16[2,64,4096]{2,1,0:T(8,128)(2,1)S(1)}, u32[]{:S(2)}, u32[]{:S(2)}) collective-permute-start(bf16[2,64,4096]{2,1,0:T(8,128)(2,1)S(1)} %get-tuple-element.42), channel_id=1, source_target_pairs={{0,4},{2,6},{4,0},{6,2},{8,12},{10,14},{12,8},{14,10},{16,20},{18,... | collective-permute-start | bytes 3145736 | tf_op jit(solution)/shard_map/ppermute | solution.py:24
  213.9 245.6 %collective-permute-start.15 = (bf16[8,64,1024]{2,1,0:T(8,128)(2,1)}, bf16[8,64,1024]{2,1,0:T(8,128)(2,1)}, u32[]{:S(2)}, u32[]{:S(2)}) collective-permute-start(bf16[8,64,1024]{2,1,0:T(8,128)(2,1)} %bitcast.54), channel_id=1, source_target_pairs={{0,16},{2,18},{4,20},{6,22},{8,24},{10,26},{12,28},{14,30},{16,0},... | collective-permute-start | bytes 3145736 | tf_op jit(solution)/shard_map/ppermute | solution.py:24
  213.9 136.6 %collective-permute-start.7 = (bf16[8,64,1024]{2,1,0:T(8,128)(2,1)S(1)}, bf16[8,64,1024]{2,1,0:T(8,128)(2,1)S(1)}, u32[]{:S(2)}, u32[]{:S(2)}) collective-permute-start(bf16[8,64,1024]{2,1,0:T(8,128)(2,1)S(1)} %bitcast.288), channel_id=1, source_target_pairs={{0,16},{2,18},{4,20},{6,22},{8,24},{10,26},{12,28},{14,30},{16,0},... | collective-permute-start | bytes 3145736 | tf_op jit(solution)/shard_map/ppermute | solution.py:24
  218.2 192.9 %collective-permute-start.3 = (bf16[8,64,1024]{2,1,0:T(8,128)(2,1)}, bf16[8,64,1024]{2,1,0:T(8,128)(2,1)}, u32[]{:S(2)}, u32[]{:S(2)}) collective-permute-start(bf16[8,64,1024]{2,1,0:T(8,128)(2,1)} %bitcast.12), channel_id=1, source_target_pairs={{0,16},{2,18},{4,20},{6,22},{8,24},{10,26},{12,28},{14,30},{16,0},... | collective-permute-start | bytes 3145736 | tf_op jit(solution)/shard_map/ppermute | solution.py:24
  219.6 176.0 %collective-permute-start.11 = (bf16[8,64,1024]{2,1,0:T(8,128)(2,1)}, bf16[8,64,1024]{2,1,0:T(8,128)(2,1)}, u32[]{:S(2)}, u32[]{:S(2)}) collective-permute-start(bf16[8,64,1024]{2,1,0:T(8,128)(2,1)} %bitcast.38), channel_id=1, source_target_pairs={{0,16},{2,18},{4,20},{6,22},{8,24},{10,26},{12,28},{14,30},{16,0},... | collective-permute-start | bytes 3145736 | tf_op jit(solution)/shard_map/ppermute | solution.py:24
  225.1 221.0 %collective-permute-start.18 = (bf16[4,64,4096]{2,1,0:T(8,128)(2,1)S(1)}, bf16[4,64,4096]{2,1,0:T(8,128)(2,1)}, u32[]{:S(2)}, u32[]{:S(2)}) collective-permute-start(bf16[4,64,4096]{2,1,0:T(8,128)(2,1)S(1)} %bitcast.284), channel_id=1, source_target_pairs={{0,8},{2,10},{4,12},{6,14},{8,0},{10,2},{12,4},{14,6},{16,24},{18,... | collective-permute-start | bytes 6291464 | tf_op jit(solution)/shard_map/ppermute | solution.py:24
  350.5 89.9 %collective-permute-start.22 = (bf16[4,64,4096]{2,1,0:T(8,128)(2,1)}, bf16[4,64,4096]{2,1,0:T(8,128)(2,1)}, u32[]{:S(2)}, u32[]{:S(2)}) collective-permute-start(bf16[4,64,4096]{2,1,0:T(8,128)(2,1)} %bitcast.81), channel_id=1, source_target_pairs={{0,8},{2,10},{4,12},{6,14},{8,0},{10,2},{12,4},{14,6},{16,24},{18,... | collective-permute-start | bytes 6291464 | tf_op jit(solution)/shard_map/ppermute | solution.py:24
  446.1 272.5 %collective-permute-start.23 = (bf16[8,64,4096]{2,1,0:T(8,128)(2,1)}, bf16[8,64,4096]{2,1,0:T(8,128)(2,1)}, u32[]{:S(2)}, u32[]{:S(2)}) collective-permute-start(bf16[8,64,4096]{2,1,0:T(8,128)(2,1)} %bitcast.84), channel_id=1, source_target_pairs={{0,16},{2,18},{4,20},{6,22},{8,24},{10,26},{12,28},{14,30},{16,0},... | collective-permute-start | bytes 12582920 | tf_op jit(solution)/shard_map/ppermute | solution.py:24
  451.2 357.2 %collective-permute-start.19 = (bf16[8,64,4096]{2,1,0:T(8,128)(2,1)}, bf16[8,64,4096]{2,1,0:T(8,128)(2,1)}, u32[]{:S(2)}, u32[]{:S(2)}) collective-permute-start(bf16[8,64,4096]{2,1,0:T(8,128)(2,1)} %bitcast.68), channel_id=1, source_target_pairs={{0,16},{2,18},{4,20},{6,22},{8,24},{10,26},{12,28},{14,30},{16,0},... | collective-permute-start | bytes 12582920 | tf_op jit(solution)/shard_map/ppermute | solution.py:24
  464.5 425.6 %copy-start.3 = (f32[640,1024]{1,0:T(8,128)}, f32[640,1024]{1,0:T(8,128)S(1)}, u32[]{:S(2)}) copy-start(f32[640,1024]{1,0:T(8,128)S(1)} %get-tuple-element.75) | copy-start | bytes 7864324
  921.5 273.4 %reduce-scatter.9.cloned.1.call-start = ((), (), s32[]{:S(2)}) async-start(), calls=%async_computation.7 | async-start | bytes 2162688 | tf_op jit(solution)/shard_map/reduce_scatter | solution.py:63
  958.8 373.1 %reduce-scatter.7.cloned.1.call-start = ((), (), s32[]{:S(2)}) async-start(), calls=%async_computation.6 | async-start | bytes 2162688 | tf_op jit(solution)/shard_map/reduce_scatter | solution.py:63
  973.2 495.8 %reduce-scatter.13.cloned.1.call-start = ((), (), s32[]{:S(2)}) async-start(), calls=%async_computation.9 | async-start | bytes 2162688 | tf_op jit(solution)/shard_map/reduce_scatter | solution.py:63
  978.7 638.7 %reduce-scatter.15.cloned.1.call-start = ((), (), s32[]{:S(2)}) async-start(), calls=%async_computation.10 | async-start | bytes 8650752 | tf_op jit(solution)/shard_map/reduce_scatter | solution.py:63
  997.4 768.5 %reduce-scatter.17.cloned.1.call-start = ((), (), s32[]{:S(2)}) async-start(), calls=%async_computation.11 | async-start | bytes 8650752 | tf_op jit(solution)/shard_map/reduce_scatter | solution.py:63
  (44 other events, 389.8 us)
Sparse Core Ops, SparseCore 0:
  921.6 136.1 reduce-scatter.10
  1060.1 134.6 reduce-scatter.8
  1197.1 134.7 reduce-scatter.6
  1334.0 134.9 reduce-scatter.12
  1471.1 146.2 reduce-scatter.14
  1619.6 146.3 reduce-scatter.16
